TPU v7x, 128 devices: a whole 4x4x4 slice. The times are simulated.
128 devices in a mesh: row: 16 (over z_hi, x, core), col: 8 (over y, z_lo).
Axes of the slice: x: 4, y: 4, z: 4 (z_hi: 2, z_lo: 2; z = z_hi * 2 + z_lo), core: 2. Of those that a mesh axis runs over, the one named last changes fastest.
Arguments:
- pair: bfloat16 [512, 512, 128], P('row', 'col'), may hold values from -6 to 6
- cotangent: bfloat16 [512, 512, 128], P('row', 'col'), may hold values from -6 to 6
- length: int32 [1], replicated, may hold values from 256 to 512
- norm_gain: float32 [128], replicated, may hold values from 0.1 to 1.9
- norm_bias: float32 [128], replicated, may hold values from -1.5 to 1.5
- left_weight: bfloat16 [128, 256], replicated, may hold values from -0.5 to 0.5
- right_weight: bfloat16 [128, 256], replicated, may hold values from -0.5 to 0.5
- gate_weight: bfloat16 [128, 128], replicated, may hold values from -0.5 to 0.5
- out_gain: float32 [128], replicated, may hold values from 0.1 to 1.9
- out_bias: float32 [128], replicated, may hold values from -2 to 2
- out_weight: bfloat16 [128, 128], replicated, may hold values from -0.5 to 0.5
Outputs:
- update: bfloat16 [512, 512, 128], P('row', 'col')
- grad_pair: bfloat16 [512, 512, 128], P('row', 'col')
- grad_left: float32 [128, 256], replicated
- grad_right: float32 [128, 256], replicated
- grad_gating: float32 [128, 128], replicated
- grad_output: float32 [128, 128], replicated
- grad_norms: float32 [4, 128], replicated
Inputs may be any that keep to these rules, and one draw needn't show every extreme that they name: Tokens at positions 511 down to length are padding.
All inputs are finite; a program needn't handle non-finite values.
Results may differ from a plain program's by a relative error of at most 0.014.
Values may be sent and summed in bfloat16 or wider, within the bound.
A program may use at most 128 MiB of HBM per device.

v0:
```python
import jax
import jax.numpy as jnp
from jax import lax
from jax.sharding import PartitionSpec as P

EPS = 1e-05


def broadcast(block, axis, holder):
    block = jnp.where(lax.axis_index(axis) == holder, block, jnp.zeros_like(block))
    return lax.psum(block, axis)


def split_up(x, dim, peers):
    dims = x.shape
    tiles = x.reshape(*dims[:dim], peers, dims[dim] // peers, *dims[dim + 1 :])
    return jnp.moveaxis(tiles, dim, 0)


def summed_on_arrival(x, axis, dim):
    peers = lax.axis_size(axis)
    tiles = lax.all_to_all(split_up(x, dim, peers), axis, 0, 0, tiled=True)
    return jnp.sum(tiles.astype(jnp.float32), axis=0)


def together(arrays, axis):
    flat, at, done = (jnp.concatenate([a.reshape(-1) for a in arrays]), 0, [])
    total = lax.psum(flat, axis)
    for a in arrays:
        done.append(total[at : at + a.size].reshape(a.shape))
        at += a.size
    return tuple(done)


def normalize(values):
    center = values - jnp.mean(values, axis=-1, keepdims=True)
    inverse = lax.rsqrt(jnp.mean(center * center, axis=-1, keepdims=True) + EPS)
    return (center * inverse, inverse)


def gating(panel, weight, first_ok, second_ok, hidden):
    projected = jnp.einsum("ikc,ch->ikh", panel, weight, preferred_element_type=jnp.float32)
    values = projected[..., :hidden]
    sigmoid_val = jax.nn.sigmoid(projected[..., hidden:])
    pad_mask = (first_ok[:, None] & second_ok[None, :]).astype(jnp.float32)[..., None]
    return ((pad_mask * sigmoid_val * values).astype(jnp.bfloat16), values, sigmoid_val, pad_mask)


def push_back(partial_value, values, sigmoid_val, pad_mask, weight, panel):
    combined = jnp.concatenate(
        [
            partial_value * pad_mask * sigmoid_val,
            partial_value * pad_mask * values * sigmoid_val * (1.0 - sigmoid_val),
        ],
        axis=-1,
    ).astype(jnp.bfloat16)
    panel_grad = jnp.einsum("ikh,ch->ikc", combined, weight, preferred_element_type=jnp.float32)
    weight_grad = jnp.einsum("ikc,ikh->ch", panel, combined, preferred_element_type=jnp.float32)
    return (panel_grad, weight_grad)


def per_device(
    pair,
    cotangent,
    length,
    norm_gain,
    norm_bias,
    left_weight,
    right_weight,
    gate_weight,
    out_gain,
    out_bias,
    out_weight,
):
    row_index = lax.axis_index("row")
    col_index = lax.axis_index("col")
    n_row = lax.axis_size("row")
    n_col = lax.axis_size("col")
    per_col = n_row // n_col
    rows_dev = pair.shape[0]
    cols_dev = pair.shape[1]
    tokens = rows_dev * n_row
    hidden = out_weight.shape[0]
    pair_hat, pair_scale = normalize(pair.astype(jnp.float32))
    normed = (pair_hat * norm_gain + norm_bias).astype(jnp.bfloat16)
    real_count = length[0]
    second_ok = jnp.arange(tokens, dtype=jnp.int32) < real_count
    own_ok = row_index * rows_dev + jnp.arange(rows_dev, dtype=jnp.int32) < real_count
    partner_ok = col_index * cols_dev + jnp.arange(cols_dev, dtype=jnp.int32) < real_count
    left_tile, left_val, left_sig, tile_mask = gating(
        normed, left_weight, own_ok, partner_ok, hidden
    )
    right_tile, right_val, right_sig, unused_mask = gating(
        normed, right_weight, own_ok, partner_ok, hidden
    )
    row_panel = lax.all_gather(normed, "col", axis=1, tiled=True)
    pieces = []
    for member in range(per_col):
        pieces.append(broadcast(row_panel, "row", col_index * per_col + member))
    col_panel = jnp.concatenate(pieces, axis=0)
    left_act = gating(row_panel, left_weight, own_ok, second_ok, hidden)[0]
    right_act = gating(col_panel, right_weight, partner_ok, second_ok, hidden)[0]
    tri = jnp.einsum("ikh,jkh->ijh", left_act, right_act, preferred_element_type=jnp.float32)
    tri_hat, tri_scale = normalize(tri)
    tri_normed = (tri_hat * out_gain + out_bias).astype(jnp.bfloat16)
    outer_val = jnp.einsum(
        "ijh,hc->ijc", tri_normed, out_weight, preferred_element_type=jnp.float32
    )
    gate_val = jax.nn.sigmoid(
        jnp.einsum("ijc,cd->ijd", normed, gate_weight, preferred_element_type=jnp.float32)
    )
    update = (gate_val * outer_val).astype(jnp.bfloat16)
    upstream = cotangent.astype(jnp.float32)
    outer_grad = (upstream * gate_val).astype(jnp.bfloat16)
    gate_grad = (upstream * outer_val * gate_val * (1.0 - gate_val)).astype(jnp.bfloat16)
    grad_output = jnp.einsum(
        "ijh,ijc->hc", tri_normed, outer_grad, preferred_element_type=jnp.float32
    )
    grad_gating = jnp.einsum("ijc,ijd->cd", normed, gate_grad, preferred_element_type=jnp.float32)
    tnorm_grad = jnp.einsum(
        "ijc,hc->ijh", outer_grad, out_weight, preferred_element_type=jnp.float32
    )
    hat_grad = tnorm_grad * out_gain
    tri_grad = (
        tri_scale
        * (
            hat_grad
            - jnp.mean(hat_grad, axis=-1, keepdims=True)
            - tri_hat * jnp.mean(hat_grad * tri_hat, axis=-1, keepdims=True)
        )
    ).astype(jnp.bfloat16)
    row_partial = jnp.einsum(
        "ijh,jkh->ikh", tri_grad, right_act, preferred_element_type=jnp.float32
    )
    col_partial = jnp.einsum("ijh,ikh->jkh", tri_grad, left_act, preferred_element_type=jnp.float32)
    row_part = summed_on_arrival(row_partial.astype(jnp.bfloat16), "col", 1)
    summed = lax.psum_scatter(
        col_partial.astype(jnp.bfloat16), "row", scatter_dimension=0, tiled=True
    )
    slab = summed[None]
    received = lax.all_to_all(slab, "col", split_axis=2, concat_axis=0, tiled=True)
    select = (jnp.arange(per_col, dtype=jnp.int32) == row_index // n_col).astype(jnp.bfloat16)
    spread = (received[:, None] * select[None, :, None, None, None]).reshape(
        (n_row,) + received.shape[1:]
    )
    returned = lax.all_to_all(spread, "row", split_axis=0, concat_axis=0, tiled=True)
    start = row_index % per_col * n_col
    owned = lax.dynamic_slice_in_dim(returned, start, n_col, 0).reshape(rows_dev, cols_dev, -1)
    col_part = owned.astype(jnp.float32)
    from_rows, grad_left = push_back(row_part, left_val, left_sig, tile_mask, left_weight, normed)
    from_cols, grad_right = push_back(
        col_part, right_val, right_sig, tile_mask, right_weight, normed
    )
    gate_back = jnp.einsum(
        "ijd,cd->ijc", gate_grad, gate_weight, preferred_element_type=jnp.float32
    )
    normed_grad = gate_back + from_rows + from_cols
    scaled = normed_grad * norm_gain
    grad_pair = (
        pair_scale
        * (
            scaled
            - jnp.mean(scaled, axis=-1, keepdims=True)
            - pair_hat * jnp.mean(scaled * pair_hat, axis=-1, keepdims=True)
        )
    ).astype(jnp.bfloat16)
    grad_norms = jnp.stack(
        [
            jnp.sum(normed_grad * pair_hat, axis=(0, 1)),
            jnp.sum(normed_grad, axis=(0, 1)),
            jnp.sum(tnorm_grad * tri_hat, axis=(0, 1)),
            jnp.sum(tnorm_grad, axis=(0, 1)),
        ]
    )
    totals = together((grad_left, grad_right, grad_gating, grad_output, grad_norms), ("row", "col"))
    inverse = 1.0 / tokens
    return (
        update,
        grad_pair,
        totals[0] * inverse,
        totals[1] * inverse,
        totals[2] * inverse,
        totals[3] * inverse,
        totals[4] * inverse,
    )


def solution(mesh):
    return jax.shard_map(
        per_device,
        mesh=mesh,
        in_specs=(
            P("row", "col", None),
            P("row", "col", None),
            P(),
            P(),
            P(),
            P(),
            P(),
            P(),
            P(),
            P(),
            P(),
        ),
        out_specs=(P("row", "col", None), P("row", "col", None), P(), P(), P(), P(), P()),
        check_vma=False,
    )
```

profile of v0, /device:TPU:1, one launch (start us, length us, event | category | flops | bytes accessed | tf_op | source)
XLA Modules:
  0.0 731.4 jit_solution(15539498948825562416)
XLA Ops:
  7.2 1.4 convert_reduce_fusion.1
  8.6 1.7 fusion.33
  10.3 2.5 fusion.27
  12.9 92.9 %all-gather.2.cloned.1.call-done = bf16[32,512,128]{2,1,0:T(8,128)(2,1)} async-done(((bf16[32,64,128]{2,1,0:T(8,128)(2,1)}), bf16[32,512,128]{2,1,0:T(8,128)(2,1)}) %all-gather.2.cloned.1.call-update) | async-done | bytes 4194320 | tf_op jit(solution)/shard_map/all_gather | solution.py:96
  105.7 5.9 broadcast_select_fusion.1
  112.5 0.2 copy-done.5
  112.7 0.4 fusion.19
  113.2 1.4 fusion.78
  114.6 3.1 copy.55
  117.7 0.1 and_convert_fusion.1
  117.7 0.1 and_convert_fusion
  117.8 4.5 fusion.57
  122.3 4.4 fusion.5
  126.7 8.0 %copy.53 = bf16[32,512,128]{1,0,2:T(8,128)(2,1)} copy(bf16[32,512,128]{2,1,0:T(8,128)(2,1)} %fusion.5) | data formatting | bytes 8388608 | tf_op jit(solution)/shard_map/convert_element_type | solution.py:46
  134.7 140.6 %all-reduce.6.cloned.1.call-done = (bf16[32,512,128]{2,1,0:T(8,128)(2,1)}, bf16[32,512,128]{2,1,0:T(8,128)(2,1)}) async-done(((bf16[32,512,128]{2,1,0:T(8,128)(2,1)}, bf16[32,512,128]{2,1,0:T(8,128)(2,1)}), (bf16[32,512,128]{2,1,0:T(8,128)(2,1)}, bf16[32,512,128]{2,1,0:T(8,128)(2,1)})) %all-reduce.6.cloned.1.call-update) | async-done | bytes 8388624 | tf_op jit(solution)/shard_map/psum | solution.py:11
  275.3 19.0 %fusion.10 = f32[64,512,256]{2,1,0:T(8,128)} fusion(bf16[32,512,128]{2,1,0:T(8,128)(2,1)} %get-tuple-element.14, bf16[32,512,128]{2,1,0:T(8,128)(2,1)} %get-tuple-element.15, bf16[128,256]{1,0:T(8,128)(2,1)S(1)} %copy-done), kind=kOutput, calls=%fused_computation.14 | convolution fusion | flops 2151677952 | bytes 42008576 | tf_op jit(solution)/shard_map/ikc,ch->ikh/dot_general | solution.py:42
  294.3 16.2 %fusion = bf16[64,512,128]{2,1,0:T(8,128)(2,1)} fusion(f32[64,512,256]{2,1,0:T(8,128)} %fusion.10, f32[64,512]{1,0:T(8,128)S(1)} %and_convert_fusion), kind=kLoop, calls=%fused_computation.1 | loop fusion | flops 25165824 | bytes 42074112 | tf_op jit(solution)/shard_map/convert_element_type | solution.py:46
  310.6 12.5 %copy.52 = bf16[64,512,128]{1,0,2:T(8,128)(2,1)} copy(bf16[64,512,128]{2,1,0:T(8,128)(2,1)} %fusion) | data formatting | bytes 16777216 | tf_op jit(solution)/shard_map/convert_element_type | solution.py:46
  323.1 6.9 bitcast_reduce_fusion
  330.0 0.3 multiply_reduce_fusion.2
  330.4 1.3 multiply_reduce_fusion
  331.7 1.9 multiply_convert_fusion
  333.5 1.0 copy-done.2
  334.5 5.6 convert_bitcast_fusion
  340.1 13.0 %copy.60 = bf16[64,512,128]{2,1,0:T(8,128)(2,1)} copy(bf16[64,512,128]{1,0,2:T(8,128)(2,1)} %convert_bitcast_fusion) | data formatting | bytes 16777216 | tf_op jit(solution)/shard_map/convert_element_type | solution.py:138
  353.1 102.8 %reduce-scatter.2.cloned.1.call-done = bf16[4,512,128]{2,1,0:T(8,128)(2,1)} async-done(((bf16[64,512,128]{2,1,0:T(8,128)(2,1)}), bf16[4,512,128]{2,1,0:T(8,128)(2,1)}) %reduce-scatter.2.cloned.1.call-update) | async-done | bytes 524304 | tf_op jit(solution)/shard_map/reduce_scatter | solution.py:137
  455.9 2.2 copy.61
  458.2 4.1 all-to-all-start.1
  462.2 6.6 convert_bitcast_fusion.1
  468.9 7.9 %copy.57 = bf16[32,512,128]{2,1,0:T(8,128)(2,1)} copy(bf16[32,512,128]{1,0,2:T(8,128)(2,1)} %convert_bitcast_fusion.1) | data formatting | bytes 8388608 | tf_op jit(solution)/shard_map/convert_element_type | solution.py:136
  476.7 5.5 copy.58
  482.2 5.3 all-to-all-start
  487.5 0.1 mul.280
  487.6 1.7 fusion.55
  489.4 1.8 fusion.60
  491.2 1.4 bitcast_multiply_fusion
  492.6 53.0 %all-to-all-done = bf16[8,32,64,128]{3,2,1,0:T(8,128)(2,1)} async-done(((bf16[8,32,64,128]{3,2,1,0:T(8,128)(2,1)}), bf16[8,32,64,128]{3,2,1,0:T(8,128)(2,1)}, u32[]{:S(2)}, u32[]{:S(2)}) %all-to-all-start) | async-done | bytes 4194336 | tf_op jit(solution)/shard_map/all_to_all | solution.py:22
  545.6 7.4 %all-to-all-start.2 = ((bf16[16,4,64,128]{3,2,1,0:T(8,128)(2,1)}), bf16[16,4,64,128]{3,2,1,0:T(8,128)(2,1)}, u32[]{:S(2)}, u32[]{:S(2)}) async-start(bf16[16,4,64,128]{3,2,1,0:T(8,128)(2,1)} %bitcast_multiply_fusion), calls=%async_computation.3 | async-start | bytes 2097152 | tf_op jit(solution)/shard_map/all_to_all | solution.py:146
  553.0 0.3 all-reduce.4.cloned.1.call-start
  553.2 0.1 and_convert_fusion.2
  553.3 2.2 copy.54
  555.5 1.2 fusion.36
  556.8 0.8 copy-done.10
  557.5 1.3 fusion.67
  558.8 4.1 convert_reduce_fusion
  563.0 7.4 %all-to-all-done.2 = bf16[16,4,64,128]{3,2,1,0:T(8,128)(2,1)} async-done(((bf16[16,4,64,128]{3,2,1,0:T(8,128)(2,1)}), bf16[16,4,64,128]{3,2,1,0:T(8,128)(2,1)}, u32[]{:S(2)}, u32[]{:S(2)}) %all-to-all-start.2) | async-done | bytes 1048608 | tf_op jit(solution)/shard_map/all_to_all | solution.py:146
  570.3 1.1 constant_dynamic-slice_fusion
  571.4 3.0 fusion.51
  574.5 0.4 convolution_bitcast_fusion.2
  574.9 0.4 convolution_bitcast_fusion.3
  575.4 0.7 constant_dynamic-update-slice_fusion.2
  576.0 0.7 constant_dynamic-update-slice_fusion.1
  576.7 1.0 fusion.15
  577.7 1.0 fusion.14
  578.6 0.4 convolution_add_fusion.1
  579.1 1.2 fusion.32
  580.3 0.6 constant_dynamic-update-slice_fusion
  580.9 2.0 fusion.31
  582.9 136.8 %all-reduce.4.cloned.1.call-done = f32[98816]{0:T(1024)} async-done(((f32[98816]{0:T(1024)}), f32[98816]{0:T(1024)}) %all-reduce.4.cloned.1.call-update) | async-done | bytes 395280 | tf_op jit(solution)/shard_map/psum | solution.py:28
  719.7 1.0 slice_multiply_fusion.4
  720.7 0.7 mul.297
  721.4 0.7 mul.299
  722.1 1.5 fusion.52
  723.6 1.3 fusion.70
  (56 shorter events, 0.6 us)
Async XLA Ops:
  7.2 268.1 %copy-start = (bf16[128,256]{1,0:T(8,128)(2,1)S(1)}, bf16[128,256]{1,0:T(8,128)(2,1)}, u32[]{:S(2)}) copy-start(bf16[128,256]{1,0:T(8,128)(2,1)} %param.17) | copy-start | bytes 196612
  7.2 98.6 %all-gather.2.cloned.1.call-start = ((), (), s32[]{:S(2)}) async-start(), calls=%async_computation.4 | async-start | bytes 4718592 | tf_op jit(solution)/shard_map/all_gather | solution.py:96
  12.8 262.5 %all-reduce.6.cloned.1.call-start = ((), (), s32[]{:S(2)}) async-start(), calls=%async_computation.7 | async-start | bytes 16777216 | tf_op jit(solution)/shard_map/psum | solution.py:11
  111.7 1.0 copy-start.5
  111.7 1.0 copy-start.14
  111.7 1.4 copy-start.7
  111.7 1.4 copy-start.13
  111.7 344.2 %reduce-scatter.2.cloned.1.call-start = ((), (), s32[]{:S(2)}) async-start(), calls=%async_computation.5 | async-start | bytes 8912896 | tf_op jit(solution)/shard_map/reduce_scatter | solution.py:137
  112.7 5.1 copy-start.12
  323.1 7.3 copy-start.16
  330.0 1.7 copy-start.17
  331.6 2.9 copy-start.1
  333.5 1.0 copy-start.2
  353.1 109.2 %copy-start.3 = (bf16[32,64,128]{1,0,2:T(8,128)(2,1)S(1)}, bf16[32,64,128]{1,0,2:T(8,128)(2,1)}, u32[]{:S(2)}) copy-start(bf16[32,64,128]{1,0,2:T(8,128)(2,1)} %copy-done.2) | copy-start | bytes 1572868
  458.2 24.1 %all-to-all-start.1 = ((bf16[1,4,512,128]{3,1,0,2:T(4,128)(2,1)}), bf16[1,4,512,128]{3,1,0,2:T(4,128)(2,1)S(1)}, u32[]{:S(2)}, u32[]{:S(2)}) async-start(bf16[1,4,512,128]{3,1,0,2:T(4,128)(2,1)} %copy.61), calls=%async_computation.2 | async-start | bytes 1048576 | tf_op jit(solution)/shard_map/all_to_all | solution.py:141
  482.2 5.4 copy-start.6
  482.2 63.3 %all-to-all-start = ((bf16[8,32,64,128]{3,2,1,0:T(8,128)(2,1)}), bf16[8,32,64,128]{3,2,1,0:T(8,128)(2,1)}, u32[]{:S(2)}, u32[]{:S(2)}) async-start(bf16[8,32,64,128]{3,2,1,0:T(8,128)(2,1)} %copy.58), calls=%async_computation | async-start | bytes 8388608 | tf_op jit(solution)/shard_map/all_to_all | solution.py:22
  489.4 66.2 %copy-start.8 = (bf16[32,64,128]{2,1,0:T(8,128)(2,1)S(1)}, bf16[32,64,128]{2,1,0:T(8,128)(2,1)}, u32[]{:S(2)}) copy-start(bf16[32,64,128]{2,1,0:T(8,128)(2,1)} %param.12) | copy-start | bytes 1572868
  545.6 24.7 %all-to-all-start.2 = ((bf16[16,4,64,128]{3,2,1,0:T(8,128)(2,1)}), bf16[16,4,64,128]{3,2,1,0:T(8,128)(2,1)}, u32[]{:S(2)}, u32[]{:S(2)}) async-start(bf16[16,4,64,128]{3,2,1,0:T(8,128)(2,1)} %bitcast_multiply_fusion), calls=%async_computation.3 | async-start | bytes 2097152 | tf_op jit(solution)/shard_map/all_to_all | solution.py:146
  553.0 166.8 %all-reduce.4.cloned.1.call-start = ((), (), s32[]{:S(2)}) async-start(), calls=%async_computation.6 | async-start | bytes 794624 | tf_op jit(solution)/shard_map/psum | solution.py:28
  556.8 0.8 copy-start.10
  574.4 2.2 copy-start.11
  574.5 4.2 copy-start.9
  574.9 4.2 copy-start.4
  574.9 4.2 copy-start.15
Sparse Core Ops, SparseCore 0:
  12.9 92.7 all-gather.1
  111.8 163.4 all-reduce.5
  353.2 102.6 reduce-scatter.1
  581.0 138.6 all-reduce.3
where the time goes:
time: 733 us; the launch traced here: 731 us
  waiting for transfers between devices  533 us (73%)
  local copies, waits for them, and re-layouts  60.6 us (8%)
  matrix products  54.7 us (7%)
  other arithmetic  50.7 us (7%)
  starting transfers between devices  17.1 us (2%)
  between operations  14.8 us (2%)
    psum x1, waiting for transfers between devices, broadcast(): return lax.psum(block, axis)  141 us
    psum x1, waiting for transfers between devices, together(): total = lax.psum(flat, axis)  137 us
    reduce_scatter x1, waiting for transfers between devices, per_device(): lax.psum_scatter(col_partial.astype(jnp.bfloat16), 'row', scatter_dimensi...  103 us
    all_gather x1, waiting for transfers between devices, per_device(): row_panel = lax.all_gather(normed, 'col', axis=1, tiled=True)  92.9 us
    all_to_all x1, waiting for transfers between devices, summed_on_arrival(): tiles = lax.all_to_all(split_up(x, dim, peers), axis, 0, 0, tiled=True)  53 us
    dot_general x4, matrix products, gating(): jnp.einsum('ikc,ch->ikh', panel, weight, preferred_element_type=jnp.float32)  27.1 us
    convert_element_type x2, other arithmetic, gating(): (pad_mask * sigmoid_val * values).astype(jnp.bfloat16)  20.6 us
    convert_element_type x2, local copies, waits for them, and re-layouts, gating(): (pad_mask * sigmoid_val * values).astype(jnp.bfloat16)  20.5 us
  transfers between devices with their start and end apart: 7, of which 6 were waited for; matrix products, arithmetic and copies ran while one was open for 8% of the time, Pallas kernels for 0%

commit v1 on v0

--- a/solution.py
+++ b/solution.py
@@ -93,7 +93,10 @@
     right_tile, right_val, right_sig, unused_mask = gating(
         normed, right_weight, own_ok, partner_ok, hidden
     )
-    row_panel = lax.all_gather(normed, "col", axis=1, tiled=True)
+    size = lax.axis_size("col")
+    blocks = jnp.stack([normed for _ in range(size)])
+    blocks = lax.all_to_all(blocks, "col", split_axis=0, concat_axis=0)
+    row_panel = jnp.concatenate(blocks, axis=1)
     pieces = []
     for member in range(per_col):
         pieces.append(broadcast(row_panel, "row", col_index * per_col + member))

time: 733 us -> 710 us (0.969)
  waiting for transfers between devices: 533 us -> 500 us
    all_gather x1 -> x0, waiting for transfers between devices: 92.9 us -> none  [per_device(): row_panel = lax.all_gather(normed, 'col', axis=1, tiled=True)]
    all_to_all x0 -> x1, waiting for transfers between devices: none -> 58.9 us  [per_device(): blocks = lax.all_to_all(blocks, 'col', split_axis=0, concat_axis=0)]
where the time goes in v1:
time: 710 us; the launch traced here: 708 us
  waiting for transfers between devices  500 us (70%)
  local copies, waits for them, and re-layouts  66.6 us (9%)
  matrix products  54.7 us (8%)
  other arithmetic  48.4 us (7%)
  starting transfers between devices  23.6 us (3%)
  between operations  14.8 us (2%)
    psum x1, waiting for transfers between devices, broadcast(): return lax.psum(block, axis)  141 us
    psum x1, waiting for transfers between devices, together(): total = lax.psum(flat, axis)  137 us
    reduce_scatter x1, waiting for transfers between devices, per_device(): lax.psum_scatter(col_partial.astype(jnp.bfloat16), 'row', scatter_dimensi...  103 us
    all_to_all x1, waiting for transfers between devices, per_device(): blocks = lax.all_to_all(blocks, 'col', split_axis=0, concat_axis=0)  58.9 us
    all_to_all x1, waiting for transfers between devices, summed_on_arrival(): tiles = lax.all_to_all(split_up(x, dim, peers), axis, 0, 0, tiled=True)  53 us
    dot_general x4, matrix products, gating(): jnp.einsum('ikc,ch->ikh', panel, weight, preferred_element_type=jnp.float32)  27.1 us
    convert_element_type x2, other arithmetic, gating(): (pad_mask * sigmoid_val * values).astype(jnp.bfloat16)  20.6 us
    convert_element_type x2, local copies, waits for them, and re-layouts, gating(): (pad_mask * sigmoid_val * values).astype(jnp.bfloat16)  20.5 us
  transfers between devices with their start and end apart: 7, of which 6 were waited for; matrix products, arithmetic and copies ran while one was open for 8% of the time, Pallas kernels for 0%

profile of v1, /device:TPU:1, one launch (start us, length us, event | category | flops | bytes accessed | tf_op | source)
XLA Modules:
  0.0 707.9 jit_solution(12645153200186953904)
XLA Ops:
  7.2 1.4 convert_reduce_fusion.1
  8.6 1.7 fusion.33
  10.3 1.7 fusion.27
  12.0 3.0 stack.12
  15.0 6.4 all-to-all-start
  21.5 58.9 %all-to-all-done = bf16[8,32,64,128]{3,2,1,0:T(8,128)(2,1)} async-done(((bf16[8,32,64,128]{3,2,1,0:T(8,128)(2,1)}), bf16[8,32,64,128]{3,2,1,0:T(8,128)(2,1)}, u32[]{:S(2)}, u32[]{:S(2)}) %all-to-all-start) | async-done | bytes 4194336 | tf_op jit(solution)/shard_map/all_to_all | solution.py:98
  80.4 3.1 copy.53
  83.6 4.4 broadcast_select_fusion.1
  88.1 0.2 reduce-scatter.2.cloned.1.call-start
  89.0 0.4 fusion.19
  89.4 1.4 fusion.78
  90.8 3.1 copy.57
  94.1 4.5 fusion.57
  98.6 4.4 fusion.5
  103.0 8.0 %copy.55 = bf16[32,512,128]{1,0,2:T(8,128)(2,1)} copy(bf16[32,512,128]{2,1,0:T(8,128)(2,1)} %fusion.5) | data formatting | bytes 8388608 | tf_op jit(solution)/shard_map/convert_element_type | solution.py:46
  111.0 141.0 %all-reduce.6.cloned.1.call-done = (bf16[32,512,128]{2,1,0:T(8,128)(2,1)}, bf16[32,512,128]{2,1,0:T(8,128)(2,1)}) async-done(((bf16[32,512,128]{2,1,0:T(8,128)(2,1)}, bf16[32,512,128]{2,1,0:T(8,128)(2,1)}), (bf16[32,512,128]{2,1,0:T(8,128)(2,1)}, bf16[32,512,128]{2,1,0:T(8,128)(2,1)})) %all-reduce.6.cloned.1.call-update) | async-done | bytes 8388624 | tf_op jit(solution)/shard_map/psum | solution.py:11
  252.0 19.0 %fusion.10 = f32[64,512,256]{2,1,0:T(8,128)} fusion(bf16[32,512,128]{2,1,0:T(8,128)(2,1)} %get-tuple-element.14, bf16[32,512,128]{2,1,0:T(8,128)(2,1)} %get-tuple-element.15, bf16[128,256]{1,0:T(8,128)(2,1)S(1)} %copy-done), kind=kOutput, calls=%fused_computation.14 | convolution fusion | flops 2151677952 | bytes 42008576 | tf_op jit(solution)/shard_map/ikc,ch->ikh/dot_general | solution.py:42
  271.0 16.2 %fusion = bf16[64,512,128]{2,1,0:T(8,128)(2,1)} fusion(f32[64,512,256]{2,1,0:T(8,128)} %fusion.10, f32[64,512]{1,0:T(8,128)S(1)} %and_convert_fusion), kind=kLoop, calls=%fused_computation.1 | loop fusion | flops 25165824 | bytes 42074112 | tf_op jit(solution)/shard_map/convert_element_type | solution.py:46
  287.2 12.5 %copy.54 = bf16[64,512,128]{1,0,2:T(8,128)(2,1)} copy(bf16[64,512,128]{2,1,0:T(8,128)(2,1)} %fusion) | data formatting | bytes 16777216 | tf_op jit(solution)/shard_map/convert_element_type | solution.py:46
  299.8 6.9 bitcast_reduce_fusion
  306.7 0.3 multiply_reduce_fusion.2
  307.0 1.3 multiply_reduce_fusion
  308.3 1.9 multiply_convert_fusion
  310.2 1.0 copy-done.3
  311.2 5.6 convert_bitcast_fusion
  316.8 13.0 %copy.62 = bf16[64,512,128]{2,1,0:T(8,128)(2,1)} copy(bf16[64,512,128]{1,0,2:T(8,128)(2,1)} %convert_bitcast_fusion) | data formatting | bytes 16777216 | tf_op jit(solution)/shard_map/convert_element_type | solution.py:141
  329.8 102.8 %reduce-scatter.2.cloned.1.call-done = bf16[4,512,128]{2,1,0:T(8,128)(2,1)} async-done(((bf16[64,512,128]{2,1,0:T(8,128)(2,1)}), bf16[4,512,128]{2,1,0:T(8,128)(2,1)}) %reduce-scatter.2.cloned.1.call-update) | async-done | bytes 524304 | tf_op jit(solution)/shard_map/reduce_scatter | solution.py:140
  432.6 2.2 copy.63
  434.8 4.1 all-to-all-start.2
  438.9 6.6 convert_bitcast_fusion.1
  445.5 7.9 %copy.59 = bf16[32,512,128]{2,1,0:T(8,128)(2,1)} copy(bf16[32,512,128]{1,0,2:T(8,128)(2,1)} %convert_bitcast_fusion.1) | data formatting | bytes 8388608 | tf_op jit(solution)/shard_map/convert_element_type | solution.py:139
  453.4 5.5 copy.60
  458.9 5.3 all-to-all-start.1
  464.2 0.1 mul.280
  464.3 1.7 fusion.55
  466.0 1.8 fusion.60
  467.9 1.4 bitcast_multiply_fusion
  469.2 53.0 %all-to-all-done.1 = bf16[8,32,64,128]{3,2,1,0:T(8,128)(2,1)} async-done(((bf16[8,32,64,128]{3,2,1,0:T(8,128)(2,1)}), bf16[8,32,64,128]{3,2,1,0:T(8,128)(2,1)}, u32[]{:S(2)}, u32[]{:S(2)}) %all-to-all-start.1) | async-done | bytes 4194336 | tf_op jit(solution)/shard_map/all_to_all | solution.py:22
  522.2 7.4 %all-to-all-start.3 = ((bf16[16,4,64,128]{3,2,1,0:T(8,128)(2,1)}), bf16[16,4,64,128]{3,2,1,0:T(8,128)(2,1)}, u32[]{:S(2)}, u32[]{:S(2)}) async-start(bf16[16,4,64,128]{3,2,1,0:T(8,128)(2,1)} %bitcast_multiply_fusion), calls=%async_computation.4 | async-start | bytes 2097152 | tf_op jit(solution)/shard_map/all_to_all | solution.py:149
  529.6 0.3 all-reduce.4.cloned.1.call-start
  530.0 2.2 copy.56
  532.2 1.2 fusion.36
  533.4 0.8 copy-done.11
  534.2 1.3 fusion.67
  535.5 4.1 convert_reduce_fusion
  539.7 7.3 %all-to-all-done.3 = bf16[16,4,64,128]{3,2,1,0:T(8,128)(2,1)} async-done(((bf16[16,4,64,128]{3,2,1,0:T(8,128)(2,1)}), bf16[16,4,64,128]{3,2,1,0:T(8,128)(2,1)}, u32[]{:S(2)}, u32[]{:S(2)}) %all-to-all-start.3) | async-done | bytes 1048608 | tf_op jit(solution)/shard_map/all_to_all | solution.py:149
  547.0 1.1 constant_dynamic-slice_fusion
  548.0 3.0 fusion.51
  551.1 0.4 convolution_bitcast_fusion.2
  551.6 0.4 convolution_bitcast_fusion.3
  552.0 0.7 constant_dynamic-update-slice_fusion.2
  552.7 0.7 constant_dynamic-update-slice_fusion.1
  553.3 1.0 fusion.15
  554.3 1.0 fusion.14
  555.3 0.4 convolution_add_fusion.1
  555.7 1.2 fusion.32
  556.9 0.6 constant_dynamic-update-slice_fusion
  557.6 2.0 fusion.31
  559.5 136.7 %all-reduce.4.cloned.1.call-done = f32[98816]{0:T(1024)} async-done(((f32[98816]{0:T(1024)}), f32[98816]{0:T(1024)}) %all-reduce.4.cloned.1.call-update) | async-done | bytes 395280 | tf_op jit(solution)/shard_map/psum | solution.py:28
  696.3 1.0 slice_multiply_fusion.4
  697.2 0.7 mul.297
  697.9 0.7 mul.299
  698.6 1.5 fusion.52
  700.2 1.3 fusion.70
  (59 shorter events, 0.8 us)
Async XLA Ops:
  7.2 244.8 %copy-start = (bf16[128,256]{1,0:T(8,128)(2,1)S(1)}, bf16[128,256]{1,0:T(8,128)(2,1)}, u32[]{:S(2)}) copy-start(bf16[128,256]{1,0:T(8,128)(2,1)} %param.17) | copy-start | bytes 196612
  12.0 77.0 %copy-start.6 = (bf16[32,64,128]{2,1,0:T(8,128)(2,1)}, bf16[32,64,128]{2,1,0:T(8,128)(2,1)S(1)}, u32[]{:S(2)}) copy-start(bf16[32,64,128]{2,1,0:T(8,128)(2,1)S(1)} %fusion.27) | copy-start | bytes 1572868
  15.0 65.4 %all-to-all-start = ((bf16[8,32,64,128]{3,2,1,0:T(8,128)(2,1)}), bf16[8,32,64,128]{3,2,1,0:T(8,128)(2,1)}, u32[]{:S(2)}, u32[]{:S(2)}) async-start(bf16[8,32,64,128]{3,2,1,0:T(8,128)(2,1)} %stack.12), calls=%async_computation | async-start | bytes 8388608 | tf_op jit(solution)/shard_map/all_to_all | solution.py:98
  21.4 230.6 %all-reduce.6.cloned.1.call-start = ((), (), s32[]{:S(2)}) async-start(), calls=%async_computation.7 | async-start | bytes 16777216 | tf_op jit(solution)/shard_map/psum | solution.py:11
  83.5 4.5 copy-start.1
  88.0 0.9 copy-start.15
  88.1 1.4 copy-start.8
  88.1 1.4 copy-start.14
  88.1 344.5 %reduce-scatter.2.cloned.1.call-start = ((), (), s32[]{:S(2)}) async-start(), calls=%async_computation.5 | async-start | bytes 8912896 | tf_op jit(solution)/shard_map/reduce_scatter | solution.py:140
  89.0 5.1 copy-start.13
  299.8 7.3 %copy-start.17 = (f32[128]{0:T(128)S(1)}, f32[128]{0:T(128)}, u32[]{:S(2)}) copy-start(f32[128]{0:T(128)} %param.19) | copy-start | bytes 1540
  306.7 1.7 copy-start.18
  308.3 2.9 copy-start.2
  310.2 1.0 copy-start.3
  329.8 109.1 %copy-start.4 = (bf16[32,64,128]{1,0,2:T(8,128)(2,1)S(1)}, bf16[32,64,128]{1,0,2:T(8,128)(2,1)}, u32[]{:S(2)}) copy-start(bf16[32,64,128]{1,0,2:T(8,128)(2,1)} %copy-done.3) | copy-start | bytes 1572868
  434.8 24.1 %all-to-all-start.2 = ((bf16[1,4,512,128]{3,1,0,2:T(4,128)(2,1)}), bf16[1,4,512,128]{3,1,0,2:T(4,128)(2,1)S(1)}, u32[]{:S(2)}, u32[]{:S(2)}) async-start(bf16[1,4,512,128]{3,1,0,2:T(4,128)(2,1)} %copy.63), calls=%async_computation.3 | async-start | bytes 1048576 | tf_op jit(solution)/shard_map/all_to_all | solution.py:144
  458.9 5.4 copy-start.7
  458.9 63.3 %all-to-all-start.1 = ((bf16[8,32,64,128]{3,2,1,0:T(8,128)(2,1)}), bf16[8,32,64,128]{3,2,1,0:T(8,128)(2,1)}, u32[]{:S(2)}, u32[]{:S(2)}) async-start(bf16[8,32,64,128]{3,2,1,0:T(8,128)(2,1)} %copy.60), calls=%async_computation.1 | async-start | bytes 8388608 | tf_op jit(solution)/shard_map/all_to_all | solution.py:22
  466.0 66.2 %copy-start.9 = (bf16[32,64,128]{2,1,0:T(8,128)(2,1)S(1)}, bf16[32,64,128]{2,1,0:T(8,128)(2,1)}, u32[]{:S(2)}) copy-start(bf16[32,64,128]{2,1,0:T(8,128)(2,1)} %param.12) | copy-start | bytes 1572868
  522.2 24.8 %all-to-all-start.3 = ((bf16[16,4,64,128]{3,2,1,0:T(8,128)(2,1)}), bf16[16,4,64,128]{3,2,1,0:T(8,128)(2,1)}, u32[]{:S(2)}, u32[]{:S(2)}) async-start(bf16[16,4,64,128]{3,2,1,0:T(8,128)(2,1)} %bitcast_multiply_fusion), calls=%async_computation.4 | async-start | bytes 2097152 | tf_op jit(solution)/shard_map/all_to_all | solution.py:149
  529.6 166.7 %all-reduce.4.cloned.1.call-start = ((), (), s32[]{:S(2)}) async-start(), calls=%async_computation.6 | async-start | bytes 794624 | tf_op jit(solution)/shard_map/psum | solution.py:28
  533.4 0.8 copy-start.11
  551.1 2.2 copy-start.12
  551.1 4.2 copy-start.10
  551.5 4.2 copy-start.5
  551.6 4.2 copy-start.16
Sparse Core Ops, SparseCore 0:
  88.2 163.7 all-reduce.5
  329.9 102.6 reduce-scatter.1
  557.7 138.5 all-reduce.3
